TPU v7x, 32 devices: a whole 2x2x4 slice. The times are simulated.
32 devices in a mesh: grp: 2 (over x), exp: 16 (over z, y, core).
Axes of the slice: x: 2, y: 2, z: 4, core: 2. Of those that a mesh axis runs over, the one named last changes fastest.
Arguments:
- tokens: bfloat16 [192, 196, 768], P(('grp', 'exp')), parts along dimension 0, may hold values from -6 to 6
- logits: float32 [192, 196, 16], P(('grp', 'exp')), parts along dimension 0, may hold values from -8 to 400
- slot_out: bfloat16 [32, 96, 768], P(('grp', 'exp')), parts along dimension 0, may hold values from -1.5 to 1.5
- slot_in: bfloat16 [32, 96, 768], P(('grp', 'exp')), parts along dimension 0, may hold values from -6 to 6
- out_grad: bfloat16 [192, 196, 768], P(('grp', 'exp')), parts along dimension 0, may hold values from -192 to 192
- router: bfloat16 [16, 768], replicated, may hold values from -0.21875 to 0.21875
- w_in: bfloat16 [16, 768, 3072], P('exp'), may hold values from -0.21875 to 0.21875
- bias_in: float32 [16, 3072], P('exp'), may hold values from -5 to 5
- w_out: bfloat16 [16, 3072, 768], P('exp'), may hold values from -0.109375 to 0.109375
Outputs:
- input_grad: bfloat16 [192, 196, 768], P(('grp', 'exp')), parts along dimension 0
- router_grad: float32 [32, 768], P(('grp', 'exp')), parts along dimension 0
There are 2 independent parts, one for each index of `grp`. A program takes and returns all parts, laid end to end along the dimension named above; an argument that names none is the same for every part. Nothing has to cross between parts.
All inputs are finite; a program needn't handle non-finite values.
Results may differ from a plain program's by a relative error of at most 0.0075.
Values may be sent and summed in bfloat16 or wider, within the bound.
A program may use at most 64 MiB of HBM per device.

v0:
```python
import functools

import jax
import jax.numpy as jnp
from jax import lax
from jax.experimental import pallas as pl
from jax.experimental.pallas import tpu as pltpu
from jax.sharding import PartitionSpec as P

gelu_root = 0.7978845608028654
gelu_cubic = 0.044715
MESH = pl.DeviceIdType.MESH
F32 = jnp.float32
BF16 = jnp.bfloat16


def gelu_slope(values):
    square = values * values
    inner_arg = gelu_root * (values + gelu_cubic * square * values)
    tanh_val = jnp.tanh(inner_arg)
    return 0.5 * (1.0 + tanh_val) + 0.5 * values * (1.0 - tanh_val * tanh_val) * gelu_root * (
        1.0 + 3.0 * gelu_cubic * square
    )


def dot(a, b):
    return lax.dot_general(a, b, (((1,), (0,)), ((), ())), preferred_element_type=F32)


def dot_nt(a, b):
    return lax.dot_general(a, b, (((1,), (1,)), ((), ())), preferred_element_type=F32)


def dot_tn(a, b):
    return lax.dot_general(a, b, (((0,), (0,)), ((), ())), preferred_element_type=F32)


def ones_where(rows, cols, wanted):
    r = lax.broadcasted_iota(jnp.int32, (rows, cols), 0)
    c = lax.broadcasted_iota(jnp.int32, (rows, cols), 1)
    return jnp.where(wanted(r, c), 1.0, 0.0).astype(BF16)


def body(
    n, b, pad, chunk,
    tok_hbm, log_hbm, so_hbm, si_hbm, og_hbm, rt_hbm, wi_hbm, bi_hbm, wo_hbm,
    ig_ref, rg_ref,
    tok, logv, so, si, og, rt, wi, bi, wo,
    comb, disp, combl, displ, slope, sg, sip,
    send_s, recv_s, send_a, recv_a, send_b, recv_b, send_r, recv_r, tok_t, pre, wi_t,
    load_sem, sem_a, sem_s, sem_b, sem_r,
):
    me = lax.axis_index("exp")
    width = tok.shape[2]
    hidden = wi.shape[2]
    rows = n * b
    padded = n * pad

    loads = {}
    pairs = [
        ("log", log_hbm, logv), ("og", og_hbm, og), ("so", so_hbm, so), ("si", si_hbm, si),
        ("wi", wi_hbm, wi), ("bi", bi_hbm, bi), ("wo", wo_hbm, wo), ("tok", tok_hbm, tok), ("rt", rt_hbm, rt),
    ]
    for at, (name, src, dst) in enumerate(pairs):
        loads[name] = pltpu.make_async_copy(src, dst, load_sem.at[at])
        loads[name].start()

    if pad != b:
        for ref in (recv_s, recv_a, recv_b):
            ref[...] = jnp.zeros_like(ref)

    barrier = pltpu.get_barrier_semaphore()

    def greet(d, _):
        peer = lax.rem(me + d, n)
        pl.semaphore_signal(barrier, inc=1, device_id={"exp": peer}, device_id_type=MESH)
        return 0

    lax.fori_loop(1, n, greet, 0, unroll=True)

    def remote(src, dst, sems, peer):
        return pltpu.make_async_remote_copy(
            src_ref=src.at[peer, :rows_of(src)], dst_ref=dst.at[me, :rows_of(src)], send_sem=sems.at[0],
            recv_sem=sems.at[1], device_id={"exp": peer}, device_id_type=MESH,
        )

    def rows_of(ref):
        return min(b, ref.shape[1])

    def send_all(src, dst, sems):
        def step(k, _):
            away = n // 2 + (k // 2) * (1 - 2 * (k % 2))
            remote(src, dst, sems, lax.rem(me + away, n)).start()
            return 0

        lax.fori_loop(1, n, step, 0, unroll=True)
        dst[me] = src[me]

    def everything(src, dst, sems):
        return pltpu.make_async_remote_copy(
            src_ref=src.at[:n - 1, :rows_of(src)], dst_ref=dst.at[:n - 1, :rows_of(src)], send_sem=sems.at[0],
            recv_sem=sems.at[1], device_id={"exp": lax.rem(me + 1, n)}, device_id_type=MESH,
        )

    def wait_all(src, dst, sems):
        everything(src, dst, sems).wait_recv()

    def drain(src, dst, sems):
        everything(src, dst, sems).wait_send()

    spread = ones_where(padded, rows, lambda r, c: (r % pad < b) & (c == (r // pad) * b + r % pad))
    to_peers = ones_where(padded, rows, lambda r, c: (r % pad < b) & (c == (r % pad) * n + r // pad))
    to_images = ones_where(rows, padded, lambda r, c: c == (r % n) * pad + r // n)

    def grouped(x):
        return x.reshape(n, pad, x.shape[1]).astype(BF16)

    def flat(x):
        return x.astype(F32).reshape(padded, x.shape[2]).astype(BF16)

    loads["log"].wait()
    loads["og"].wait()
    for i in range(b):
        lt = logv[i]
        e = jnp.exp(lt - jnp.max(lt, axis=0, keepdims=True))
        c = e / jnp.sum(e, axis=0, keepdims=True)
        comb[i] = c
        sg[i * n:(i + 1) * n, :] = dot(c.astype(BF16), og[i]).astype(BF16)
    send_a[...] = grouped(dot(to_peers, sg[...]))
    pl.semaphore_wait(barrier, n - 1)
    send_all(send_a, recv_a, sem_a)
    loads["so"].wait()
    send_s[...] = grouped(dot(spread, so[0]))
    send_all(send_s, recv_s, sem_s)

    for i in range(b):
        lt = logv[i]
        e = jnp.exp(lt - jnp.max(lt, axis=1, keepdims=True))
        disp[i] = e / jnp.sum(e, axis=1, keepdims=True)

    loads["si"].wait()
    sip[...] = dot(spread, si[0]).astype(BF16)
    loads["wi"].wait()
    loads["bi"].wait()
    for k in range(0, hidden, chunk):
        hp = dot(sip[...], wi[0, :, k:k + chunk]) + bi[:, k:k + chunk]
        slope[:, k:k + chunk] = gelu_slope(hp)
        wi_t[k:k + chunk, :] = wi[0, :, k:k + chunk].T

    loads["wo"].wait()
    wait_all(send_a, recv_a, sem_a)
    got = flat(recv_a[...])
    for k in range(0, hidden, chunk):
        hg = dot_nt(got, wo[0, k:k + chunk, :])
        pre[:, k:k + chunk] = (hg * slope[:, k:k + chunk]).astype(BF16)
    blocks, block = send_b.shape[0], send_b.shape[3]
    for q in range(blocks):
        acc = dot(pre[...], wi_t[:, q * block:(q + 1) * block])
        send_b[q] = grouped(acc)
        send_all(send_b.at[q], recv_b.at[q], sem_b.at[q])

    loads["tok"].wait()
    loads["rt"].wait()
    wait_all(send_s, recv_s, sem_s)
    outs = dot(to_images, flat(recv_s[...])).astype(BF16)
    racc = jnp.zeros((n, width), F32)
    for i in range(b):
        cg = dot_nt(outs[i * n:(i + 1) * n, :], og[i])
        c = comb[i]
        cl = (c * (cg - jnp.sum(c * cg, axis=0, keepdims=True))).astype(BF16)
        combl[i] = cl
        racc = racc + dot(cl, tok[i])
        tok_t[i] = tok[i].T

    for q in range(blocks):
        wait_all(send_b.at[q], recv_b.at[q], sem_b.at[q])
        sg[:, q * block:(q + 1) * block] = dot(to_images, flat(recv_b[q])).astype(BF16)
    for i in range(b):
        dg = dot(sg[i * n:(i + 1) * n, :], tok_t[i])
        d = disp[i]
        dl = (d * (dg - jnp.sum(d * dg, axis=1, keepdims=True))).astype(BF16)
        displ[i] = dl
        racc = racc + dot(dl, tok[i])
    send_r[...] = racc.reshape(n, 1, width)
    send_all(send_r, recv_r, sem_r)

    for i in range(b):
        left = jnp.concatenate([disp[i].astype(BF16), combl[i], displ[i]], axis=0)
        right = jnp.concatenate([sg[i * n:(i + 1) * n, :], rt[...], rt[...]], axis=0)
        ig_ref[i] = dot_tn(left, right).astype(BF16)

    drain(send_s, recv_s, sem_s)
    drain(send_a, recv_a, sem_a)
    for q in range(blocks):
        drain(send_b.at[q], recv_b.at[q], sem_b.at[q])
    wait_all(send_r, recv_r, sem_r)
    rg_ref[...] = jnp.sum(recv_r[...], axis=0) / (n * b)
    drain(send_r, recv_r, sem_r)


def on_device(tokens, logits, slot_out, slot_in, out_grad, router, w_in, bias_in, w_out):
    b, seq, width = tokens.shape
    n = lax.axis_size("exp")
    hidden = w_in.shape[2]
    pad = -(-b // 8) * 8
    padded = n * pad
    chunk = 768 if hidden % 768 == 0 else hidden
    hbm_spec = pl.BlockSpec(memory_space=pltpu.HBM)
    limit = 67043328 - 65536 - b * (-(-seq // 8) * 8) * width * 2
    exchange = pltpu.VMEM((n, pad, width), BF16)
    small = pltpu.VMEM((n, 1, width), F32)
    sems = pltpu.SemaphoreType.DMA((2,))
    block = width // 2 if width % 256 == 0 else width
    columns = pltpu.VMEM((width // block, n, pad, block), BF16)
    return pl.pallas_call(
        functools.partial(body, n, b, pad, chunk),
        out_shape=(
            pltpu.VMEM((b, seq, width), BF16),
            pltpu.VMEM((1, width), F32),
        ),
        in_specs=[hbm_spec] * 9,
        out_specs=(pl.BlockSpec(memory_space=pltpu.VMEM), pl.BlockSpec(memory_space=pltpu.VMEM)),
        scratch_shapes=[
            pltpu.VMEM(tokens.shape, BF16),
            pltpu.VMEM((b, n, seq), F32),
            pltpu.VMEM(slot_out.shape, BF16),
            pltpu.VMEM(slot_in.shape, BF16),
            pltpu.VMEM(out_grad.shape, BF16),
            pltpu.VMEM(router.shape, BF16),
            pltpu.VMEM(w_in.shape, BF16),
            pltpu.VMEM(bias_in.shape, F32),
            pltpu.VMEM(w_out.shape, BF16),
            pltpu.VMEM((b, n, seq), F32),
            pltpu.VMEM((b, n, seq), F32),
            pltpu.VMEM((b, n, seq), BF16),
            pltpu.VMEM((b, n, seq), BF16),
            pltpu.VMEM((padded, hidden), F32),
            pltpu.VMEM((n * b, width), BF16),
            pltpu.VMEM((padded, width), BF16),
            exchange, exchange, exchange, exchange, columns, columns, small, small,
            pltpu.VMEM((b, width, seq), BF16),
            pltpu.VMEM((padded, hidden), BF16),
            pltpu.VMEM((hidden, width), BF16),
            pltpu.SemaphoreType.DMA((9,)),
            sems, sems, pltpu.SemaphoreType.DMA((width // block, 2)), sems,
        ],
        compiler_params=pltpu.CompilerParams(
            collective_id=0, has_side_effects=True, vmem_limit_bytes=limit
        ),
        name="moe_input_grad",
    )(tokens, jnp.swapaxes(logits, 1, 2), slot_out, slot_in, out_grad, router, w_in, bias_in, w_out)


def solution(mesh):
    placed = (
        P(("grp", "exp"), None, None),
        P(("grp", "exp"), None, None),
        P(("grp", "exp"), None, None),
        P(("grp", "exp"), None, None),
        P(("grp", "exp"), None, None),
        P(),
        P("exp", None, None),
        P("exp", None),
        P("exp", None, None),
    )
    return jax.shard_map(
        on_device,
        mesh=mesh,
        in_specs=placed,
        out_specs=(P(("grp", "exp"), None, None), P(("grp", "exp"), None)),
        check_vma=False,
    )
```

profile of v0, /device:TPU:0, one launch (start us, length us, event | category | flops | bytes accessed | tf_op | source)
XLA Modules:
  0.0 28.4 jit_solution(16907320997111294046)
XLA Ops:
  0.6 25.9 %moe_input_grad.1 = (bf16[6,196,768]{2,1,0:T(8,128)(2,1)S(1)}, f32[1,768]{1,0:T(1,128)S(1)}) custom-call(bf16[6,196,768]{2,1,0:T(8,128)(2,1)} %tok_hbm.1, f32[6,16,196]{2,1,0:T(8,128)} %bitcast.1, bf16[1,96,768]{2,1,0:T(8,128)(2,1)} %so_hbm.1, bf16[1,96,768]{2,1,0:T(8,128)(2,1)} %si_hbm.1, bf16[6,196,768]{2,1,0:T(8,128)(2,1)} %og_hbm.1, ...), custom_call_target="tpu_custom_call" | custom-call | tf_op jit(solution)/shard_map/moe_input_grad/pallas_call | solution.py:215
  26.6 1.2 %copy.13 = bf16[6,196,768]{2,1,0:T(8,128)(2,1)} copy(bf16[6,196,768]{2,1,0:T(8,128)(2,1)S(1)} %get-tuple-element.2) | data formatting | bytes 3612672
  27.8 0.6 %copy.14 = f32[1,768]{1,0:T(1,128)} copy(f32[1,768]{1,0:T(1,128)S(1)} %get-tuple-element.3) | data formatting | bytes 6144
where the time goes:
time: 28.5 us; the launch traced here: 28.4 us
  Pallas kernels  25.9 us (91%)
  local copies, waits for them, and re-layouts  1.81 us (6%)
  between operations  0.64 us (2%)
    pallas_call x1, Pallas kernels, on_device(): pl.pallas_call(functools.partial(body, n, b, pad, chunk), out_shape=(pltp...  25.9 us
    unnamed x2, local copies, waits for them, and re-layouts  1.81 us

commit v1 on v0

v1 whole, which is shorter than its diff:
```python
import functools

import jax
import jax.numpy as jnp
from jax import lax
from jax.experimental import pallas as pl
from jax.experimental.pallas import tpu as pltpu
from jax.sharding import PartitionSpec as P

gelu_root = 0.7978845608028654
gelu_cubic = 0.044715
MESH = pl.DeviceIdType.MESH
F32 = jnp.float32
BF16 = jnp.bfloat16


def gelu_slope(values):
    square = values * values
    inner_arg = gelu_root * (values + gelu_cubic * square * values)
    tanh_val = jnp.tanh(inner_arg)
    return 0.5 * (1.0 + tanh_val) + 0.5 * values * (1.0 - tanh_val * tanh_val) * gelu_root * (
        1.0 + 3.0 * gelu_cubic * square
    )


def dot(a, b):
    return lax.dot_general(a, b, (((1,), (0,)), ((), ())), preferred_element_type=F32)


def dot_nt(a, b):
    return lax.dot_general(a, b, (((1,), (1,)), ((), ())), preferred_element_type=F32)


def dot_tn(a, b):
    return lax.dot_general(a, b, (((0,), (0,)), ((), ())), preferred_element_type=F32)


def ones_where(rows, cols, wanted):
    r = lax.broadcasted_iota(jnp.int32, (rows, cols), 0)
    c = lax.broadcasted_iota(jnp.int32, (rows, cols), 1)
    return jnp.where(wanted(r, c), 1.0, 0.0).astype(BF16)


def body(
    n, b, pad, chunk, tile, cuts,
    tok_hbm, log_hbm, so_hbm, si_hbm, og_hbm, rt_hbm, wi_hbm, bi_hbm, wo_hbm,
    ig_ref, rg_ref,
    tok, logv, so, si, og, rt, wi, bi, wo,
    comb, disp, combl, displ, slope, sg, sip, rsum, part, dgs,
    send_s, recv_s, send_a, recv_a, send_b, recv_b, send_r, recv_r, tok_t, pre, wi_t, wo_t,
    load_sem, sem_a, sem_s, sem_b, sem_r,
):
    me = lax.axis_index("exp")
    width = tok.shape[2]
    hidden = wi.shape[2]
    rows = n * b
    padded = n * pad

    barrier = pltpu.get_barrier_semaphore()

    def greet(d, _):
        peer = lax.rem(me + d, n)
        pl.semaphore_signal(barrier, inc=1, device_id={"exp": peer}, device_id_type=MESH)
        return 0

    lax.fori_loop(1, n, greet, 0, unroll=True)

    loads = {}
    pairs = [
        ("log", log_hbm, logv), ("og", og_hbm, og), ("si", si_hbm, si),
        ("wi", wi_hbm, wi), ("bi", bi_hbm, bi), ("wo", wo_hbm, wo), ("so", so_hbm, so), ("tok", tok_hbm, tok),
        ("rt", rt_hbm, rt),
    ]
    for at, (name, src, dst) in enumerate(pairs):
        loads[name] = pltpu.make_async_copy(src, dst, load_sem.at[at])
        loads[name].start()

    def view(ref, at, cut):
        rows_sent = min(b, ref.shape[1])
        return ref.at[at, :rows_sent, cut[0]:cut[1]]

    lone = jnp.abs(n - 1 - 2 * me)

    def far_first(k):
        pair = jnp.maximum(k - lone, 0)
        step = jnp.minimum(me, n - 1 - me) - pair // 2
        end = jnp.where(me < n // 2, n - 1 - k, k)
        return jnp.where(k < lone, end, me + step * (1 - 2 * (pair % 2)))

    def send_all(src, dst, sems, cut):
        def step(k, _):
            peer = far_first(k)
            pltpu.make_async_remote_copy(
                src_ref=view(src, peer, cut), dst_ref=view(dst, me, cut), send_sem=sems.at[0],
                recv_sem=sems.at[1], device_id={"exp": peer}, device_id_type=MESH,
            ).start()
            return 0

        lax.fori_loop(0, n - 1, step, 0, unroll=True)
        dst[me, :, cut[0]:cut[1]] = src[me, :, cut[0]:cut[1]]

    def everything(src, dst, sems, cut):
        return pltpu.make_async_remote_copy(
            src_ref=view(src, slice(0, n - 1), cut), dst_ref=view(dst, slice(0, n - 1), cut), send_sem=sems.at[0],
            recv_sem=sems.at[1], device_id={"exp": lax.rem(me + 1, n)}, device_id_type=MESH,
        )

    def wait_all(src, dst, sems, cut):
        everything(src, dst, sems, cut).wait_recv()

    def drain(src, dst, sems, cut):
        everything(src, dst, sems, cut).wait_send()

    whole = (0, width)
    spread = ones_where(padded, rows, lambda r, c: (r % pad < b) & (c == (r // pad) * b + r % pad))
    to_peers = ones_where(padded, rows, lambda r, c: (r % pad < b) & (c == (r % pad) * n + r // pad))
    to_images = ones_where(rows, padded, lambda r, c: c == (r % n) * pad + r // n)

    def grouped(x):
        return x.reshape(n, pad, x.shape[1]).astype(BF16)

    def flat(x):
        wide = x.astype(F32)
        if pad != b:
            wide = jnp.where(lax.broadcasted_iota(jnp.int32, (1, pad, 1), 1) < b, wide, 0.0)
        return wide.reshape(padded, x.shape[2]).astype(BF16)

    def of_image(i):
        return slice(i * n, (i + 1) * n)

    loads["log"].wait()
    for i in range(b):
        lt = logv[i]
        e = jnp.exp(lt - jnp.max(lt, axis=0, keepdims=True))
        comb[i] = e / jnp.sum(e, axis=0, keepdims=True)
    loads["og"].wait()
    for i in range(b):
        sg[of_image(i), :] = dot(comb[i].astype(BF16), og[i]).astype(BF16)
    send_a[...] = grouped(dot(to_peers, sg[...]))
    pl.semaphore_wait(barrier, n - 1)
    for q, cut in enumerate(cuts):
        send_all(send_a, recv_a, sem_a.at[q], cut)

    loads["si"].wait()
    sip[...] = dot(spread, si[0]).astype(BF16)
    loads["wi"].wait()
    loads["bi"].wait()
    for k in range(0, hidden, tile):
        hp = dot(sip[...], wi[0, :, k:k + tile]) + bi[:, k:k + tile]
        slope[:, k:k + tile] = gelu_slope(hp)
        wi_t[k:k + tile, :] = wi[0, :, k:k + tile].T
    for i in range(b):
        lt = logv[i]
        e = jnp.exp(lt - jnp.max(lt, axis=1, keepdims=True))
        disp[i] = e / jnp.sum(e, axis=1, keepdims=True)
    loads["so"].wait()
    send_s[...] = grouped(dot(spread, so[0]))
    send_all(send_s, recv_s, sem_s, whole)
    loads["wo"].wait()
    for k in range(0, hidden, chunk):
        wo_t[:, k:k + chunk] = wo[0, k:k + chunk, :].T

    for q, (lo, hi) in enumerate(cuts):
        wait_all(send_a, recv_a, sem_a.at[q], (lo, hi))
        got = flat(recv_a[:, :, lo:hi])
        for k in range(0, hidden, chunk):
            hg = dot(got, wo_t[lo:hi, k:k + chunk])
            if q > 0:
                hg = hg + part[:, k:k + chunk]
            if q < len(cuts) - 1:
                part[:, k:k + chunk] = hg
            else:
                pre[:, k:k + chunk] = (hg * slope[:, k:k + chunk]).astype(BF16)
    for q, (lo, hi) in enumerate(cuts):
        send_b[:, :, lo:hi] = grouped(dot(pre[...], wi_t[:, lo:hi]))
        send_all(send_b, recv_b, sem_b.at[q], (lo, hi))

    loads["tok"].wait()
    loads["rt"].wait()
    for i in range(b):
        tok_t[i] = tok[i].T
    wait_all(send_s, recv_s, sem_s, whole)
    outs = dot(to_images, flat(recv_s[...])).astype(BF16)
    for i in range(b):
        dgs[i] = dot_nt(outs[of_image(i), :], og[i])
    for i in range(b):
        c, cg = comb[i], dgs[i]
        combl[i] = (c * (cg - jnp.sum(c * cg, axis=0, keepdims=True))).astype(BF16)
    racc = jnp.zeros((n, width), F32)
    for i in range(b):
        racc = racc + dot(combl[i], tok[i])
    rsum[...] = racc

    for q, (lo, hi) in enumerate(cuts):
        wait_all(send_b, recv_b, sem_b.at[q], (lo, hi))
        sg[:, lo:hi] = dot(to_images, flat(recv_b[:, :, lo:hi])).astype(BF16)
        for i in range(b):
            dg = dot(sg[of_image(i), lo:hi], tok_t[i, lo:hi, :])
            dgs[i] = dg if q == 0 else dgs[i] + dg
    for i in range(b):
        d, dg = disp[i], dgs[i]
        displ[i] = (d * (dg - jnp.sum(d * dg, axis=1, keepdims=True))).astype(BF16)
    racc = rsum[...]
    for i in range(b):
        racc = racc + dot(displ[i], tok[i])
    send_r[...] = racc.reshape(n, 1, width)
    send_all(send_r, recv_r, sem_r, whole)

    for i in range(b):
        left = jnp.concatenate([disp[i].astype(BF16), combl[i], displ[i]], axis=0)
        right = jnp.concatenate([sg[of_image(i), :], rt[...], rt[...]], axis=0)
        ig_ref[i] = dot_tn(left, right).astype(BF16)

    drain(send_s, recv_s, sem_s, whole)
    for q, cut in enumerate(cuts):
        drain(send_a, recv_a, sem_a.at[q], cut)
        drain(send_b, recv_b, sem_b.at[q], cut)
    wait_all(send_r, recv_r, sem_r, whole)
    rg_ref[...] = jnp.sum(recv_r[...], axis=0) / rows
    drain(send_r, recv_r, sem_r, whole)


def write_out(ig_ref, rg_ref, ig_hbm, rg_hbm, sems):
    copies = [pltpu.make_async_copy(rg_ref, rg_hbm, sems.at[0])]
    for i in range(ig_ref.shape[0]):
        copies.append(pltpu.make_async_copy(ig_ref.at[i], ig_hbm.at[i], sems.at[i + 1]))
    for copy in copies:
        copy.start()
    for copy in copies:
        copy.wait()


def on_device(tokens, logits, slot_out, slot_in, out_grad, router, w_in, bias_in, w_out):
    b, seq, width = tokens.shape
    n = lax.axis_size("exp")
    hidden = w_in.shape[2]
    pad = -(-b // 8) * 8
    padded = n * pad
    chunk = 768 if hidden % 768 == 0 else hidden
    tile = 256 if hidden % 256 == 0 else hidden
    cuts = [(0, width - 256), (width - 256, width)] if width % 256 == 0 and width > 256 else [(0, width)]
    hbm_spec = pl.BlockSpec(memory_space=pltpu.HBM)
    vmem_spec = pl.BlockSpec(memory_space=pltpu.VMEM)
    limit = 67043328 - 65536 - b * (-(-seq // 8) * 8) * width * 2
    exchange = pltpu.VMEM((n, pad, width), BF16)
    small = pltpu.VMEM((n, 1, width), F32)
    sems = pltpu.SemaphoreType.DMA((2,))
    sems_cut = pltpu.SemaphoreType.DMA((len(cuts), 2))
    ig, rg = pl.pallas_call(
        functools.partial(body, n, b, pad, chunk, tile, cuts),
        out_shape=(
            pltpu.VMEM((b, seq, width), BF16),
            pltpu.VMEM((1, width), F32),
        ),
        in_specs=[hbm_spec] * 9,
        out_specs=(vmem_spec, vmem_spec),
        scratch_shapes=[
            pltpu.VMEM(tokens.shape, BF16),
            pltpu.VMEM((b, n, seq), F32),
            pltpu.VMEM(slot_out.shape, BF16),
            pltpu.VMEM(slot_in.shape, BF16),
            pltpu.VMEM(out_grad.shape, BF16),
            pltpu.VMEM(router.shape, BF16),
            pltpu.VMEM(w_in.shape, BF16),
            pltpu.VMEM(bias_in.shape, F32),
            pltpu.VMEM(w_out.shape, BF16),
            pltpu.VMEM((b, n, seq), F32),
            pltpu.VMEM((b, n, seq), F32),
            pltpu.VMEM((b, n, seq), BF16),
            pltpu.VMEM((b, n, seq), BF16),
            pltpu.VMEM((padded, hidden), F32),
            pltpu.VMEM((n * b, width), BF16),
            pltpu.VMEM((padded, width), BF16),
            pltpu.VMEM((n, width), F32),
            pltpu.VMEM((padded, hidden), F32),
            pltpu.VMEM((b, n, seq), F32),
            exchange, exchange, exchange, exchange, exchange, exchange, small, small,
            pltpu.VMEM((b, width, seq), BF16),
            pltpu.VMEM((padded, hidden), BF16),
            pltpu.VMEM((hidden, width), BF16),
            pltpu.VMEM((width, hidden), BF16),
            pltpu.SemaphoreType.DMA((9,)),
            sems_cut, sems, sems_cut, sems,
        ],
        compiler_params=pltpu.CompilerParams(
            collective_id=0, has_side_effects=True, vmem_limit_bytes=limit
        ),
        name="moe_input_grad",
    )(tokens, jnp.swapaxes(logits, 1, 2), slot_out, slot_in, out_grad, router, w_in, bias_in, w_out)
    return pl.pallas_call(
        write_out,
        out_shape=(jax.ShapeDtypeStruct(ig.shape, BF16), jax.ShapeDtypeStruct(rg.shape, F32)),
        in_specs=[vmem_spec, vmem_spec],
        out_specs=(hbm_spec, hbm_spec),
        scratch_shapes=[pltpu.SemaphoreType.DMA((b + 1,))],
        compiler_params=pltpu.CompilerParams(vmem_limit_bytes=1 << 20),
        name="write_out",
    )(
        pltpu.with_memory_space_constraint(ig, pltpu.VMEM),
        pltpu.with_memory_space_constraint(rg, pltpu.VMEM),
    )


def solution(mesh):
    placed = (
        P(("grp", "exp"), None, None),
        P(("grp", "exp"), None, None),
        P(("grp", "exp"), None, None),
        P(("grp", "exp"), None, None),
        P(("grp", "exp"), None, None),
        P(),
        P("exp", None, None),
        P("exp", None),
        P("exp", None, None),
    )
    return jax.shard_map(
        on_device,
        mesh=mesh,
        in_specs=placed,
        out_specs=(P(("grp", "exp"), None, None), P(("grp", "exp"), None)),
        check_vma=False,
    )
```

time: 28.5 us -> 24.8 us (0.87)
  local copies, waits for them, and re-layouts: 1.81 us -> 0 us
  Pallas kernels: 25.9 us -> 24.1 us
    pallas_call x1 -> x2, Pallas kernels: 25.9 us -> 24.1 us  [the longest x1 22.8 us: on_device(): pl.pallas_call(functools.partial(body, n, b, pad, chunk, tile, cuts), out...]
    unnamed x2 -> x0, local copies, waits for them, and re-layouts: 1.81 us -> none
where the time goes in v1:
time: 24.8 us; the launch traced here: 24.7 us
  Pallas kernels  24.1 us (97%)
  between operations  0.64 us (3%)
    pallas_call x1, Pallas kernels, on_device(): pl.pallas_call(functools.partial(body, n, b, pad, chunk, tile, cuts), out...  22.8 us
    pallas_call x1, Pallas kernels, on_device(): pl.pallas_call(write_out, out_shape=(jax.ShapeDtypeStruct(ig.shape, BF16)...  1.29 us

profile of v1, /device:TPU:0, one launch (start us, length us, event | category | flops | bytes accessed | tf_op | source)
XLA Modules:
  0.0 24.7 jit_solution(1354270720646110918)
XLA Ops:
  0.6 22.8 %moe_input_grad.1 = (bf16[6,196,768]{2,1,0:T(8,128)(2,1)S(1)}, f32[1,768]{1,0:T(1,128)S(1)}) custom-call(bf16[6,196,768]{2,1,0:T(8,128)(2,1)} %tok_hbm.1, f32[6,16,196]{2,1,0:T(8,128)} %bitcast.1, bf16[1,96,768]{2,1,0:T(8,128)(2,1)} %so_hbm.1, bf16[1,96,768]{2,1,0:T(8,128)(2,1)} %si_hbm.1, bf16[6,196,768]{2,1,0:T(8,128)(2,1)} %og_hbm.1, ...), custom_call_target="tpu_custom_call" | custom-call | tf_op jit(solution)/shard_map/moe_input_grad/pallas_call | solution.py:249
  23.4 1.3 %write_out.1 = (bf16[6,196,768]{2,1,0:T(8,128)(2,1)}, f32[1,768]{1,0:T(1,128)}) custom-call(bf16[6,196,768]{2,1,0:T(8,128)(2,1)S(1)} %get-tuple-element.4.ig_ref, f32[1,768]{1,0:T(1,128)S(1)} %get-tuple-element.5.rg_ref), custom_call_target="tpu_custom_call" | custom-call | tf_op jit(solution)/shard_map/write_out/pallas_call | solution.py:290

commit v2 on v1

--- a/solution.py
+++ b/solution.py
@@ -46,7 +46,7 @@
     tok_hbm, log_hbm, so_hbm, si_hbm, og_hbm, rt_hbm, wi_hbm, bi_hbm, wo_hbm,
     ig_ref, rg_ref,
     tok, logv, so, si, og, rt, wi, bi, wo,
-    comb, disp, combl, displ, slope, sg, sip, rsum, part, dgs,
+    comb, disp, combl, displ_a, displ_b, slope, sg, sig_a, sig_b, sip, rsum, part, dgs,
     send_s, recv_s, send_a, recv_a, send_b, recv_b, send_r, recv_r, tok_t, pre, wi_t, wo_t,
     load_sem, sem_a, sem_s, sem_b, sem_r,
 ):
@@ -55,6 +55,8 @@
     hidden = wi.shape[2]
     rows = n * b
     padded = n * pad
+    sig, displ = (sig_a, sig_b), (displ_a, displ_b)
+    groups = [(0, n // 4, -(-(n // 4) // 8) * 8), (n // 4, n, n)]
 
     barrier = pltpu.get_barrier_semaphore()
 
@@ -79,25 +81,29 @@
         rows_sent = min(b, ref.shape[1])
         return ref.at[at, :rows_sent, cut[0]:cut[1]]
 
-    lone = jnp.abs(n - 1 - 2 * me)
+    g = 4 if n % 4 == 0 else 1
+    block = me // g
+    lone = jnp.abs(n // g - 1 - 2 * block)
 
     def far_first(k):
-        pair = jnp.maximum(k - lone, 0)
-        step = jnp.minimum(me, n - 1 - me) - pair // 2
-        end = jnp.where(me < n // 2, n - 1 - k, k)
-        return jnp.where(k < lone, end, me + step * (1 - 2 * (pair % 2)))
-
-    def send_all(src, dst, sems, cut):
-        def step(k, _):
+        kb, w = k // g, k % g
+        if k >= n - g:
+            return me ^ (g - 1 - w)
+        pair = jnp.maximum(kb - lone, 0)
+        step = jnp.minimum(block, n // g - 1 - block) - pair // 2
+        end = jnp.where(block < n // g // 2, n // g - 1 - kb, kb)
+        there = jnp.where(kb < lone, end, block + step * (1 - 2 * (pair % 2)))
+        return there * g + ((me % g) ^ (g - 1 - w))
+
+    def send_all(src, dst, sems, cut, first=0, last=n - 1):
+        for k in range(first, last):
             peer = far_first(k)
             pltpu.make_async_remote_copy(
                 src_ref=view(src, peer, cut), dst_ref=view(dst, me, cut), send_sem=sems.at[0],
                 recv_sem=sems.at[1], device_id={"exp": peer}, device_id_type=MESH,
             ).start()
-            return 0
-
-        lax.fori_loop(0, n - 1, step, 0, unroll=True)
-        dst[me, :, cut[0]:cut[1]] = src[me, :, cut[0]:cut[1]]
+        if last == n - 1:
+            dst[me, :, cut[0]:cut[1]] = src[me, :, cut[0]:cut[1]]
 
     def everything(src, dst, sems, cut):
         return pltpu.make_async_remote_copy(
@@ -123,7 +129,7 @@
         wide = x.astype(F32)
         if pad != b:
             wide = jnp.where(lax.broadcasted_iota(jnp.int32, (1, pad, 1), 1) < b, wide, 0.0)
-        return wide.reshape(padded, x.shape[2]).astype(BF16)
+        return wide.reshape(x.shape[0] * pad, x.shape[2]).astype(BF16)
 
     def of_image(i):
         return slice(i * n, (i + 1) * n)
@@ -139,7 +145,9 @@
     send_a[...] = grouped(dot(to_peers, sg[...]))
     pl.semaphore_wait(barrier, n - 1)
     for q, cut in enumerate(cuts):
-        send_all(send_a, recv_a, sem_a.at[q], cut)
+        send_all(send_a, recv_a, sem_a.at[q], cut, 0, n // 4)
+    for q, cut in enumerate(cuts):
+        send_all(send_a, recv_a, sem_a.at[q], cut, n // 4)
 
     loads["si"].wait()
     sip[...] = dot(spread, si[0]).astype(BF16)
@@ -171,9 +179,33 @@
                 part[:, k:k + chunk] = hg
             else:
                 pre[:, k:k + chunk] = (hg * slope[:, k:k + chunk]).astype(BF16)
+    mine = jnp.minimum(me // groups[0][1], 1)
+
+    def send_rows(q, ks):
+        lo, hi = cuts[q]
+        for k in ks:
+            peer = far_first(k)
+            pltpu.make_async_remote_copy(
+                src_ref=send_b.at[peer, :b, lo:hi], dst_ref=recv_b.at[me, :b, lo:hi], send_sem=sem_b.at[q, 0],
+                recv_sem=sem_b.at[q, 1 + mine], device_id={"exp": peer}, device_id_type=MESH,
+            ).start()
+
+    def rows_between(q, own):
+        lo, hi = cuts[q]
+        return pltpu.make_async_remote_copy(
+            src_ref=send_b.at[own, :b, lo:hi], dst_ref=recv_b.at[own, :b, lo:hi], send_sem=sem_b.at[q, 0],
+            recv_sem=sem_b.at[q, 1 + (own.start > 0)], device_id={"exp": lax.rem(me + 1, n)}, device_id_type=MESH,
+        )
+
     for q, (lo, hi) in enumerate(cuts):
         send_b[:, :, lo:hi] = grouped(dot(pre[...], wi_t[:, lo:hi]))
-        send_all(send_b, recv_b, sem_b.at[q], (lo, hi))
+        send_rows(q, range(n // 4))
+        pltpu.make_async_copy(
+            send_b.at[me, :b, lo:hi], recv_b.at[me, :b, lo:hi], sem_b.at[q, 1 + mine]
+        ).start()
+    for k in range(n // 4, n - 1):
+        for q in range(len(cuts)):
+            send_rows(q, [k])
 
     loads["tok"].wait()
     loads["rt"].wait()
@@ -191,30 +223,48 @@
         racc = racc + dot(combl[i], tok[i])
     rsum[...] = racc
 
-    for q, (lo, hi) in enumerate(cuts):
-        wait_all(send_b, recv_b, sem_b.at[q], (lo, hi))
-        sg[:, lo:hi] = dot(to_images, flat(recv_b[:, :, lo:hi])).astype(BF16)
+    for h, (lo, hi, tall) in enumerate(groups):
+        own = slice(lo, hi)
+        first = tall - (hi - lo) if h else 0
+        to_group = ones_where(
+            b * tall, (hi - lo) * pad,
+            lambda r, c: (c == (r % tall - first) * pad + r // tall) & (r % tall >= first) & (r % tall < first + hi - lo),
+        )
+        for q, (left, right) in enumerate(cuts):
+            rows_between(q, own).wait_recv()
+            got = dot(to_group, flat(recv_b[own, :, left:right]))
+            sig[h][:, :, left:right] = got.reshape(b, tall, right - left).astype(BF16)
+            for i in range(b):
+                dg = dot(sig[h][i, :, left:right], tok_t[i, left:right, :])
+                dgs[i, :tall, :] = dg if q == 0 else dgs[i, :tall, :] + dg
+        racc = rsum[:tall, :]
         for i in range(b):
-            dg = dot(sg[of_image(i), lo:hi], tok_t[i, lo:hi, :])
-            dgs[i] = dg if q == 0 else dgs[i] + dg
-    for i in range(b):
-        d, dg = disp[i], dgs[i]
-        displ[i] = (d * (dg - jnp.sum(d * dg, axis=1, keepdims=True))).astype(BF16)
-    racc = rsum[...]
-    for i in range(b):
-        racc = racc + dot(displ[i], tok[i])
-    send_r[...] = racc.reshape(n, 1, width)
-    send_all(send_r, recv_r, sem_r, whole)
-
-    for i in range(b):
-        left = jnp.concatenate([disp[i].astype(BF16), combl[i], displ[i]], axis=0)
-        right = jnp.concatenate([sg[of_image(i), :], rt[...], rt[...]], axis=0)
+            d, dg = disp[i, :tall, :], dgs[i, :tall, :]
+            dl = (d * (dg - jnp.sum(d * dg, axis=1, keepdims=True))).astype(BF16)
+            displ[h][i] = dl
+            racc = racc + dot(dl, tok[i])
+        send_r[own] = racc[lo:hi].reshape(hi - lo, 1, width)
+        for j in range(lo, hi):
+            @pl.when(me != j)
+            def _():
+                pltpu.make_async_remote_copy(
+                    src_ref=send_r.at[j], dst_ref=recv_r.at[me], send_sem=sem_r.at[0],
+                    recv_sem=sem_r.at[1], device_id={"exp": j}, device_id_type=MESH,
+                ).start()
+    recv_r[me] = send_r[me]
+
+    for i in range(b):
+        tall = groups[0][2]
+        dr = disp[i].astype(BF16)
+        left = jnp.concatenate([dr, combl[i], displ[1][i], dr[:tall], displ[0][i]], axis=0)
+        right = jnp.concatenate([sig[1][i], rt[...], rt[...], sig[0][i], rt[:tall, :]], axis=0)
         ig_ref[i] = dot_tn(left, right).astype(BF16)
 
     drain(send_s, recv_s, sem_s, whole)
     for q, cut in enumerate(cuts):
         drain(send_a, recv_a, sem_a.at[q], cut)
-        drain(send_b, recv_b, sem_b.at[q], cut)
+    for q in range(len(cuts)):
+        rows_between(q, slice(0, n - 1)).wait_send()
     wait_all(send_r, recv_r, sem_r, whole)
     rg_ref[...] = jnp.sum(recv_r[...], axis=0) / rows
     drain(send_r, recv_r, sem_r, whole)
@@ -236,6 +286,7 @@
     hidden = w_in.shape[2]
     pad = -(-b // 8) * 8
     padded = n * pad
+    early = -(-(n // 4) // 8) * 8
     chunk = 768 if hidden % 768 == 0 else hidden
     tile = 256 if hidden % 256 == 0 else hidden
     cuts = [(0, width - 256), (width - 256, width)] if width % 256 == 0 and width > 256 else [(0, width)]
@@ -245,7 +296,7 @@
     exchange = pltpu.VMEM((n, pad, width), BF16)
     small = pltpu.VMEM((n, 1, width), F32)
     sems = pltpu.SemaphoreType.DMA((2,))
-    sems_cut = pltpu.SemaphoreType.DMA((len(cuts), 2))
+    sems_cut = pltpu.SemaphoreType.DMA((2, 2))
     ig, rg = pl.pallas_call(
         functools.partial(body, n, b, pad, chunk, tile, cuts),
         out_shape=(
@@ -267,9 +318,12 @@
             pltpu.VMEM((b, n, seq), F32),
             pltpu.VMEM((b, n, seq), F32),
             pltpu.VMEM((b, n, seq), BF16),
+            pltpu.VMEM((b, early, seq), BF16),
             pltpu.VMEM((b, n, seq), BF16),
             pltpu.VMEM((padded, hidden), F32),
             pltpu.VMEM((n * b, width), BF16),
+            pltpu.VMEM((b, early, width), BF16),
+            pltpu.VMEM((b, n, width), BF16),
             pltpu.VMEM((padded, width), BF16),
             pltpu.VMEM((n, width), F32),
             pltpu.VMEM((padded, hidden), F32),
@@ -280,7 +334,7 @@
             pltpu.VMEM((hidden, width), BF16),
             pltpu.VMEM((width, hidden), BF16),
             pltpu.SemaphoreType.DMA((9,)),
-            sems_cut, sems, sems_cut, sems,
+            sems_cut, sems, pltpu.SemaphoreType.DMA((len(cuts), 3)), sems,
         ],
         compiler_params=pltpu.CompilerParams(
             collective_id=0, has_side_effects=True, vmem_limit_bytes=limit

time: 24.8 us -> 23.3 us (0.940)
  Pallas kernels: 24.1 us -> 22.5 us
    pallas_call x1, Pallas kernels: 22.8 us -> 21.2 us  [on_device(): pl.pallas_call(functools.partial(body, n, b, pad, chunk, tile, cuts), out...]
where the time goes in v2:
time: 23.3 us; the launch traced here: 23.2 us
  Pallas kernels  22.5 us (97%)
  between operations  0.64 us (3%)
    pallas_call x1, Pallas kernels, on_device(): pl.pallas_call(functools.partial(body, n, b, pad, chunk, tile, cuts), out...  21.2 us
    pallas_call x1, Pallas kernels, on_device(): pl.pallas_call(write_out, out_shape=(jax.ShapeDtypeStruct(ig.shape, BF16)...  1.29 us

profile of v2, /device:TPU:0, one launch (start us, length us, event | category | flops | bytes accessed | tf_op | source)
XLA Modules:
  0.0 23.2 jit_solution(12235295192517670061)
XLA Ops:
  0.6 21.2 %moe_input_grad.1 = (bf16[6,196,768]{2,1,0:T(8,128)(2,1)S(1)}, f32[1,768]{1,0:T(1,128)S(1)}) custom-call(bf16[6,196,768]{2,1,0:T(8,128)(2,1)} %tok_hbm.1, f32[6,16,196]{2,1,0:T(8,128)} %bitcast.1, bf16[1,96,768]{2,1,0:T(8,128)(2,1)} %so_hbm.1, bf16[1,96,768]{2,1,0:T(8,128)(2,1)} %si_hbm.1, bf16[6,196,768]{2,1,0:T(8,128)(2,1)} %og_hbm.1, ...), custom_call_target="tpu_custom_call" | custom-call | tf_op jit(solution)/shard_map/moe_input_grad/pallas_call | solution.py:300
  21.9 1.3 %write_out.1 = (bf16[6,196,768]{2,1,0:T(8,128)(2,1)}, f32[1,768]{1,0:T(1,128)}) custom-call(bf16[6,196,768]{2,1,0:T(8,128)(2,1)S(1)} %get-tuple-element.4.ig_ref, f32[1,768]{1,0:T(1,128)S(1)} %get-tuple-element.5.rg_ref), custom_call_target="tpu_custom_call" | custom-call | tf_op jit(solution)/shard_map/write_out/pallas_call | solution.py:344

commit v3 on v2

--- a/solution.py
+++ b/solution.py
@@ -46,17 +46,20 @@
     tok_hbm, log_hbm, so_hbm, si_hbm, og_hbm, rt_hbm, wi_hbm, bi_hbm, wo_hbm,
     ig_ref, rg_ref,
     tok, logv, so, si, og, rt, wi, bi, wo,
-    comb, disp, combl, displ_a, displ_b, slope, sg, sig_a, sig_b, sip, rsum, part, dgs,
+    comb, disp, combl, displ_a, displ_b, spread_disp, spread_dg, slope, sg, sig_a, sig_b, sip, rsum, part, dgs,
     send_s, recv_s, send_a, recv_a, send_b, recv_b, send_r, recv_r, tok_t, pre, wi_t, wo_t,
-    load_sem, sem_a, sem_s, sem_b, sem_r,
+    load_sem, og_sem, sem_a, sem_s, sem_b, sem_r,
 ):
     me = lax.axis_index("exp")
     width = tok.shape[2]
     hidden = wi.shape[2]
     rows = n * b
     padded = n * pad
-    sig, displ = (sig_a, sig_b), (displ_a, displ_b)
-    groups = [(0, n // 4, -(-(n // 4) // 8) * 8), (n // 4, n, n)]
+    lanes = 128
+    seq = logv.shape[2]
+    span = tok_t.shape[1] // b
+    early = n // 4
+    tall = early * pad
 
     barrier = pltpu.get_barrier_semaphore()
 
@@ -65,7 +68,8 @@
         pl.semaphore_signal(barrier, inc=1, device_id={"exp": peer}, device_id_type=MESH)
         return 0
 
-    lax.fori_loop(1, n, greet, 0, unroll=True)
+    def greet_all():
+        lax.fori_loop(1, n, greet, 0, unroll=True)
 
     loads = {}
     pairs = [
@@ -75,7 +79,20 @@
     ]
     for at, (name, src, dst) in enumerate(pairs):
         loads[name] = pltpu.make_async_copy(src, dst, load_sem.at[at])
-        loads[name].start()
+        if name == "og":
+            for i in range(b):
+                loads["og", i] = pltpu.make_async_copy(src.at[i], dst.at[i], og_sem.at[i])
+                loads["og", i].start()
+            continue
+        if at == 2:
+            greet_all()
+        if name not in ("wo", "tok", "so", "rt"):
+            loads[name].start()
+    if span != seq:
+        for i in range(b):
+            tok_t[:, i * span + seq // lanes * lanes:(i + 1) * span] = jnp.zeros(
+                (width, span - seq // lanes * lanes), BF16
+            )
 
     def view(ref, at, cut):
         rows_sent = min(b, ref.shape[1])
@@ -83,21 +100,19 @@
 
     g = 4 if n % 4 == 0 else 1
     block = me // g
-    lone = jnp.abs(n // g - 1 - 2 * block)
-
-    def far_first(k):
+
+    def peer_at(k):
         kb, w = k // g, k % g
         if k >= n - g:
             return me ^ (g - 1 - w)
-        pair = jnp.maximum(kb - lone, 0)
-        step = jnp.minimum(block, n // g - 1 - block) - pair // 2
-        end = jnp.where(block < n // g // 2, n // g - 1 - kb, kb)
-        there = jnp.where(kb < lone, end, block + step * (1 - 2 * (pair % 2)))
+        last = n // g - 1 - kb
+        there = jnp.where(last + 1 > block, last + 1, last) if kb else 0
+        there = jnp.where(block == 0, last, there)
         return there * g + ((me % g) ^ (g - 1 - w))
 
     def send_all(src, dst, sems, cut, first=0, last=n - 1):
         for k in range(first, last):
-            peer = far_first(k)
+            peer = peer_at(k)
             pltpu.make_async_remote_copy(
                 src_ref=view(src, peer, cut), dst_ref=view(dst, me, cut), send_sem=sems.at[0],
                 recv_sem=sems.at[1], device_id={"exp": peer}, device_id_type=MESH,
@@ -119,7 +134,6 @@
 
     whole = (0, width)
     spread = ones_where(padded, rows, lambda r, c: (r % pad < b) & (c == (r // pad) * b + r % pad))
-    to_peers = ones_where(padded, rows, lambda r, c: (r % pad < b) & (c == (r % pad) * n + r // pad))
     to_images = ones_where(rows, padded, lambda r, c: c == (r % n) * pad + r // n)
 
     def grouped(x):
@@ -135,39 +149,69 @@
         return slice(i * n, (i + 1) * n)
 
     loads["log"].wait()
+    loads["wo"].start()
+    loads["tok"].start()
+    loads["so"].start()
+    loads["rt"].start()
     for i in range(b):
         lt = logv[i]
         e = jnp.exp(lt - jnp.max(lt, axis=0, keepdims=True))
         comb[i] = e / jnp.sum(e, axis=0, keepdims=True)
-    loads["og"].wait()
-    for i in range(b):
-        sg[of_image(i), :] = dot(comb[i].astype(BF16), og[i]).astype(BF16)
-    send_a[...] = grouped(dot(to_peers, sg[...]))
+    for i in range(b):
+        loads["og", i].wait()
+    for i in range(b):
+        row = dot(comb[i].astype(BF16), og[i])
+        for c in range(width // lanes):
+            sg[c, pl.ds(i, n, stride=pad), :] = row[:, c * lanes:(c + 1) * lanes]
+    for c in range(width // lanes):
+        send_a[:, :, c * lanes:(c + 1) * lanes] = grouped(sg[c])
+    def prepare():
+        loads["si"].wait()
+        sip[...] = dot(spread, si[0]).astype(BF16)
+        loads["wi"].wait()
+        loads["bi"].wait()
+        for k in range(0, hidden, tile):
+            hp = dot(sip[...], wi[0, :, k:k + tile]) + bi[:, k:k + tile]
+            slope[:, k:k + tile] = gelu_slope(hp)
+            wi_t[k:k + tile, :] = wi[0, :, k:k + tile].T
+
+    pl.when(me < n // 8)(prepare)
     pl.semaphore_wait(barrier, n - 1)
     for q, cut in enumerate(cuts):
         send_all(send_a, recv_a, sem_a.at[q], cut, 0, n // 4)
     for q, cut in enumerate(cuts):
         send_all(send_a, recv_a, sem_a.at[q], cut, n // 4)
 
-    loads["si"].wait()
-    sip[...] = dot(spread, si[0]).astype(BF16)
-    loads["wi"].wait()
-    loads["bi"].wait()
-    for k in range(0, hidden, tile):
-        hp = dot(sip[...], wi[0, :, k:k + tile]) + bi[:, k:k + tile]
-        slope[:, k:k + tile] = gelu_slope(hp)
-        wi_t[k:k + tile, :] = wi[0, :, k:k + tile].T
+    pl.when(me >= n // 8)(prepare)
+
     for i in range(b):
         lt = logv[i]
         e = jnp.exp(lt - jnp.max(lt, axis=1, keepdims=True))
         disp[i] = e / jnp.sum(e, axis=1, keepdims=True)
-    loads["so"].wait()
-    send_s[...] = grouped(dot(spread, so[0]))
-    send_all(send_s, recv_s, sem_s, whole)
+    def send_slots():
+        loads["so"].wait()
+        send_s[...] = grouped(dot(spread, so[0]))
+        send_all(send_s, recv_s, sem_s, whole)
+
+    pl.when(me >= n // 8)(send_slots)
     loads["wo"].wait()
     for k in range(0, hidden, chunk):
         wo_t[:, k:k + chunk] = wo[0, k:k + chunk, :].T
 
+    def turn_tokens():
+        loads["tok"].wait()
+        loads["rt"].wait()
+        for i in range(b):
+            tok_t[:, i * span:i * span + seq] = tok[i].T
+        spread_disp[...] = jnp.zeros_like(spread_disp)
+        for i in range(b):
+            here = lax.broadcasted_iota(jnp.int32, (pad, seq), 0) == i
+            for j in range(early):
+                value = jnp.where(here, disp[i, j:j + 1, :], 0.0)
+                spread_disp[j * pad:(j + 1) * pad, i * span:i * span + seq] = value
+
+    pl.when(me < n // 8)(turn_tokens)
+    pl.when(me < n // 8)(send_slots)
     for q, (lo, hi) in enumerate(cuts):
         wait_all(send_a, recv_a, sem_a.at[q], (lo, hi))
         got = flat(recv_a[:, :, lo:hi])
@@ -179,12 +223,12 @@
                 part[:, k:k + chunk] = hg
             else:
                 pre[:, k:k + chunk] = (hg * slope[:, k:k + chunk]).astype(BF16)
-    mine = jnp.minimum(me // groups[0][1], 1)
+    mine = jnp.minimum(me // early, 1)
 
     def send_rows(q, ks):
         lo, hi = cuts[q]
         for k in ks:
-            peer = far_first(k)
+            peer = peer_at(k)
             pltpu.make_async_remote_copy(
                 src_ref=send_b.at[peer, :b, lo:hi], dst_ref=recv_b.at[me, :b, lo:hi], send_sem=sem_b.at[q, 0],
                 recv_sem=sem_b.at[q, 1 + mine], device_id={"exp": peer}, device_id_type=MESH,
@@ -207,10 +251,7 @@
         for q in range(len(cuts)):
             send_rows(q, [k])
 
-    loads["tok"].wait()
-    loads["rt"].wait()
-    for i in range(b):
-        tok_t[i] = tok[i].T
+    pl.when(me >= n // 8)(turn_tokens)
     wait_all(send_s, recv_s, sem_s, whole)
     outs = dot(to_images, flat(recv_s[...])).astype(BF16)
     for i in range(b):
@@ -218,32 +259,8 @@
     for i in range(b):
         c, cg = comb[i], dgs[i]
         combl[i] = (c * (cg - jnp.sum(c * cg, axis=0, keepdims=True))).astype(BF16)
-    racc = jnp.zeros((n, width), F32)
-    for i in range(b):
-        racc = racc + dot(combl[i], tok[i])
-    rsum[...] = racc
-
-    for h, (lo, hi, tall) in enumerate(groups):
-        own = slice(lo, hi)
-        first = tall - (hi - lo) if h else 0
-        to_group = ones_where(
-            b * tall, (hi - lo) * pad,
-            lambda r, c: (c == (r % tall - first) * pad + r // tall) & (r % tall >= first) & (r % tall < first + hi - lo),
-        )
-        for q, (left, right) in enumerate(cuts):
-            rows_between(q, own).wait_recv()
-            got = dot(to_group, flat(recv_b[own, :, left:right]))
-            sig[h][:, :, left:right] = got.reshape(b, tall, right - left).astype(BF16)
-            for i in range(b):
-                dg = dot(sig[h][i, :, left:right], tok_t[i, left:right, :])
-                dgs[i, :tall, :] = dg if q == 0 else dgs[i, :tall, :] + dg
-        racc = rsum[:tall, :]
-        for i in range(b):
-            d, dg = disp[i, :tall, :], dgs[i, :tall, :]
-            dl = (d * (dg - jnp.sum(d * dg, axis=1, keepdims=True))).astype(BF16)
-            displ[h][i] = dl
-            racc = racc + dot(dl, tok[i])
-        send_r[own] = racc[lo:hi].reshape(hi - lo, 1, width)
+
+    def send_router(lo, hi):
         for j in range(lo, hi):
             @pl.when(me != j)
             def _():
@@ -251,13 +268,60 @@
                     src_ref=send_r.at[j], dst_ref=recv_r.at[me], send_sem=sem_r.at[0],
                     recv_sem=sem_r.at[1], device_id={"exp": j}, device_id_type=MESH,
                 ).start()
+
+    for q, (lo, hi) in enumerate(cuts):
+        rows_between(q, slice(0, early)).wait_recv()
+        got = flat(recv_b[:early, :, lo:hi])
+        sig_a[:, lo:hi] = got
+        dg = dot(got, tok_t[lo:hi, :])
+        if q > 0:
+            dg = dg + spread_dg[...]
+        if q < len(cuts) - 1:
+            spread_dg[...] = dg
+    d = spread_disp[...]
+    part_sum = d * dg
+    dl = (part_sum - d * jnp.sum(part_sum, axis=1, keepdims=True)).astype(BF16)
+    displ_a[...] = dl
+    racc = jnp.zeros((n + tall, width), F32)
+    for i in range(b):
+        terms = jnp.concatenate([combl[i], dl[:, i * span:i * span + seq]], axis=0)
+        racc = racc + dot(terms, tok[i])
+    rsum[...] = racc[:n]
+    own = jnp.sum(racc[n:].reshape(early, pad, width), axis=1, keepdims=True)
+    send_r[:early] = own + racc[:early].reshape(early, 1, width)
+    send_router(0, early)
+
+    to_image_rows = ones_where(
+        rows, (n - early) * pad,
+        lambda r, c: (c == (r % n - early) * pad + r // n) & (r % n >= early),
+    )
+    for q, (lo, hi) in enumerate(cuts):
+        rows_between(q, slice(early, n)).wait_recv()
+        sig_b[:, lo:hi] = dot(to_image_rows, flat(recv_b[early:, :, lo:hi])).astype(BF16)
+        for i in range(b):
+            dg = dot(sig_b[of_image(i), lo:hi], tok_t[lo:hi, i * span:i * span + seq])
+            dgs[i] = dg if q == 0 else dgs[i] + dg
+    racc = rsum[...]
+    for i in range(b):
+        d, dg = disp[i], dgs[i]
+        dl = (d * (dg - jnp.sum(d * dg, axis=1, keepdims=True))).astype(BF16)
+        displ_b[i] = dl
+        racc = racc + dot(dl, tok[i])
+    send_r[early:] = racc[early:].reshape(n - early, 1, width)
+    send_router(early, n)
     recv_r[me] = send_r[me]
 
-    for i in range(b):
-        tall = groups[0][2]
-        dr = disp[i].astype(BF16)
-        left = jnp.concatenate([dr, combl[i], displ[1][i], dr[:tall], displ[0][i]], axis=0)
-        right = jnp.concatenate([sig[1][i], rt[...], rt[...], sig[0][i], rt[:tall, :]], axis=0)
+    spread_rt = dot(
+        ones_where(tall, n, lambda r, c: c == r // pad), rt[...]
+    ).astype(BF16)
+    for i in range(b):
+        at = slice(i * span, i * span + seq)
+        left = jnp.concatenate(
+            [spread_disp[:, at].astype(BF16), displ_a[:, at], disp[i].astype(BF16), combl[i], displ_b[i]], axis=0
+        )
+        right = jnp.concatenate(
+            [sig_a[...], spread_rt, sig_b[of_image(i), :], rt[...], rt[...]], axis=0
+        )
         ig_ref[i] = dot_tn(left, right).astype(BF16)
 
     drain(send_s, recv_s, sem_s, whole)
@@ -286,7 +350,8 @@
     hidden = w_in.shape[2]
     pad = -(-b // 8) * 8
     padded = n * pad
-    early = -(-(n // 4) // 8) * 8
+    tall = n // 4 * pad
+    span = -(-seq // 128) * 128
     chunk = 768 if hidden % 768 == 0 else hidden
     tile = 256 if hidden % 256 == 0 else hidden
     cuts = [(0, width - 256), (width - 256, width)] if width % 256 == 0 and width > 256 else [(0, width)]
@@ -318,22 +383,25 @@
             pltpu.VMEM((b, n, seq), F32),
             pltpu.VMEM((b, n, seq), F32),
             pltpu.VMEM((b, n, seq), BF16),
-            pltpu.VMEM((b, early, seq), BF16),
+            pltpu.VMEM((tall, b * span), BF16),
             pltpu.VMEM((b, n, seq), BF16),
+            pltpu.VMEM((tall, b * span), F32),
+            pltpu.VMEM((tall, b * span), F32),
             pltpu.VMEM((padded, hidden), F32),
+            pltpu.VMEM((width // 128, padded, 128), F32),
+            pltpu.VMEM((tall, width), BF16),
             pltpu.VMEM((n * b, width), BF16),
-            pltpu.VMEM((b, early, width), BF16),
-            pltpu.VMEM((b, n, width), BF16),
             pltpu.VMEM((padded, width), BF16),
             pltpu.VMEM((n, width), F32),
             pltpu.VMEM((padded, hidden), F32),
             pltpu.VMEM((b, n, seq), F32),
             exchange, exchange, exchange, exchange, exchange, exchange, small, small,
-            pltpu.VMEM((b, width, seq), BF16),
+            pltpu.VMEM((width, b * span), BF16),
             pltpu.VMEM((padded, hidden), BF16),
             pltpu.VMEM((hidden, width), BF16),
             pltpu.VMEM((width, hidden), BF16),
             pltpu.SemaphoreType.DMA((9,)),
+            pltpu.SemaphoreType.DMA((b,)),
             sems_cut, sems, pltpu.SemaphoreType.DMA((len(cuts), 3)), sems,
         ],
         compiler_params=pltpu.CompilerParams(

time: 23.3 us -> 23.7 us (1.017)
  Pallas kernels: 22.5 us -> 22.9 us
    pallas_call x1, Pallas kernels: 21.2 us -> 21.6 us  [on_device(): pl.pallas_call(functools.partial(body, n, b, pad, chunk, tile, cuts), out...]
where the time goes in v3:
time: 23.7 us; the launch traced here: 23.5 us
  Pallas kernels  22.9 us (97%)
  between operations  0.64 us (3%)
    pallas_call x1, Pallas kernels, on_device(): pl.pallas_call(functools.partial(body, n, b, pad, chunk, tile, cuts), out...  21.6 us
    pallas_call x1, Pallas kernels, on_device(): pl.pallas_call(write_out, out_shape=(jax.ShapeDtypeStruct(ig.shape, BF16)...  1.29 us

profile of v3, /device:TPU:0, one launch (start us, length us, event | category | flops | bytes accessed | tf_op | source)
XLA Modules:
  0.0 23.5 jit_solution(9104145953207446500)
XLA Ops:
  0.6 21.6 %moe_input_grad.1 = (bf16[6,196,768]{2,1,0:T(8,128)(2,1)S(1)}, f32[1,768]{1,0:T(1,128)S(1)}) custom-call(bf16[6,196,768]{2,1,0:T(8,128)(2,1)} %tok_hbm.1, f32[6,16,196]{2,1,0:T(8,128)} %bitcast.1, bf16[1,96,768]{2,1,0:T(8,128)(2,1)} %so_hbm.1, bf16[1,96,768]{2,1,0:T(8,128)(2,1)} %si_hbm.1, bf16[6,196,768]{2,1,0:T(8,128)(2,1)} %og_hbm.1, ...), custom_call_target="tpu_custom_call" | custom-call | tf_op jit(solution)/shard_map/moe_input_grad/pallas_call | solution.py:365
  22.2 1.3 %write_out.1 = (bf16[6,196,768]{2,1,0:T(8,128)(2,1)}, f32[1,768]{1,0:T(1,128)}) custom-call(bf16[6,196,768]{2,1,0:T(8,128)(2,1)S(1)} %get-tuple-element.4.ig_ref, f32[1,768]{1,0:T(1,128)S(1)} %get-tuple-element.5.rg_ref), custom_call_target="tpu_custom_call" | custom-call | tf_op jit(solution)/shard_map/write_out/pallas_call | solution.py:412

commit v4 on v3

--- a/solution.py
+++ b/solution.py
@@ -242,11 +242,14 @@
         )
 
     for q, (lo, hi) in enumerate(cuts):
-        send_b[:, :, lo:hi] = grouped(dot(pre[...], wi_t[:, lo:hi]))
-        send_rows(q, range(n // 4))
-        pltpu.make_async_copy(
-            send_b.at[me, :b, lo:hi], recv_b.at[me, :b, lo:hi], sem_b.at[q, 1 + mine]
-        ).start()
+        @pl.when(me >= 0)
+        def _():
+            send_b[:, :, lo:hi] = grouped(dot(pre[...], wi_t[:, lo:hi]))
+            send_rows(q, range(n // 4))
+            pltpu.make_async_copy(
+                send_b.at[me, :b, lo:hi], recv_b.at[me, :b, lo:hi], sem_b.at[q, 1 + mine]
+            ).start()
+
     for k in range(n // 4, n - 1):
         for q in range(len(cuts)):
             send_rows(q, [k])

time: 23.7 us -> 23.2 us (0.979)
  Pallas kernels: 22.9 us -> 22.4 us
    pallas_call x1, Pallas kernels: 21.6 us -> 21.1 us  [on_device(): pl.pallas_call(functools.partial(body, n, b, pad, chunk, tile, cuts), out...]
where the time goes in v4:
time: 23.2 us; the launch traced here: 23.1 us
  Pallas kernels  22.4 us (97%)
  between operations  0.64 us (3%)
    pallas_call x1, Pallas kernels, on_device(): pl.pallas_call(functools.partial(body, n, b, pad, chunk, tile, cuts), out...  21.1 us
    pallas_call x1, Pallas kernels, on_device(): pl.pallas_call(write_out, out_shape=(jax.ShapeDtypeStruct(ig.shape, BF16)...  1.29 us

profile of v4, /device:TPU:0, one launch (start us, length us, event | category | flops | bytes accessed | tf_op | source)
XLA Modules:
  0.0 23.1 jit_solution(1533408692134482424)
XLA Ops:
  0.6 21.1 %moe_input_grad.1 = (bf16[6,196,768]{2,1,0:T(8,128)(2,1)S(1)}, f32[1,768]{1,0:T(1,128)S(1)}) custom-call(bf16[6,196,768]{2,1,0:T(8,128)(2,1)} %tok_hbm.1, f32[6,16,196]{2,1,0:T(8,128)} %bitcast.1, bf16[1,96,768]{2,1,0:T(8,128)(2,1)} %so_hbm.1, bf16[1,96,768]{2,1,0:T(8,128)(2,1)} %si_hbm.1, bf16[6,196,768]{2,1,0:T(8,128)(2,1)} %og_hbm.1, ...), custom_call_target="tpu_custom_call" | custom-call | tf_op jit(solution)/shard_map/moe_input_grad/pallas_call | solution.py:368
  21.8 1.3 %write_out.1 = (bf16[6,196,768]{2,1,0:T(8,128)(2,1)}, f32[1,768]{1,0:T(1,128)}) custom-call(bf16[6,196,768]{2,1,0:T(8,128)(2,1)S(1)} %get-tuple-element.4.ig_ref, f32[1,768]{1,0:T(1,128)S(1)} %get-tuple-element.5.rg_ref), custom_call_target="tpu_custom_call" | custom-call | tf_op jit(solution)/shard_map/write_out/pallas_call | solution.py:415

commit v5 on v4

--- a/solution.py
+++ b/solution.py
@@ -110,9 +110,17 @@
         there = jnp.where(block == 0, last, there)
         return there * g + ((me % g) ^ (g - 1 - w))
 
-    def send_all(src, dst, sems, cut, first=0, last=n - 1):
+    def peer_upward(k):
+        kb, w = k // g, k % g
+        if k >= n - g:
+            return me ^ (g - 1 - w)
+        last = n // g - 1 - kb
+        there = jnp.where(last > block, last, last - 1)
+        return jnp.where(block < n // g // 2, there * g + ((me % g) ^ (g - 1 - w)), peer_at(k))
+
+    def send_all(src, dst, sems, cut, first=0, last=n - 1, order=peer_at):
         for k in range(first, last):
-            peer = peer_at(k)
+            peer = order(k)
             pltpu.make_async_remote_copy(
                 src_ref=view(src, peer, cut), dst_ref=view(dst, me, cut), send_sem=sems.at[0],
                 recv_sem=sems.at[1], device_id={"exp": peer}, device_id_type=MESH,
@@ -191,7 +199,7 @@
     def send_slots():
         loads["so"].wait()
         send_s[...] = grouped(dot(spread, so[0]))
-        send_all(send_s, recv_s, sem_s, whole)
+        send_all(send_s, recv_s, sem_s, whole, order=peer_upward)
 
     pl.when(me >= n // 8)(send_slots)
     loads["wo"].wait()

time: 23.2 us -> 23.2 us (level)
  no operation moved by 1% of the time
where the time goes in v5:
time: 23.2 us; the launch traced here: 23.1 us
  Pallas kernels  22.4 us (97%)
  between operations  0.64 us (3%)
    pallas_call x1, Pallas kernels, on_device(): pl.pallas_call(functools.partial(body, n, b, pad, chunk, tile, cuts), out...  21.1 us
    pallas_call x1, Pallas kernels, on_device(): pl.pallas_call(write_out, out_shape=(jax.ShapeDtypeStruct(ig.shape, BF16)...  1.29 us

profile of v5, /device:TPU:0, one launch (start us, length us, event | category | flops | bytes accessed | tf_op | source)
XLA Modules:
  0.0 23.1 jit_solution(3275454588640964953)
XLA Ops:
  0.6 21.1 %moe_input_grad.1 = (bf16[6,196,768]{2,1,0:T(8,128)(2,1)S(1)}, f32[1,768]{1,0:T(1,128)S(1)}) custom-call(bf16[6,196,768]{2,1,0:T(8,128)(2,1)} %tok_hbm.1, f32[6,16,196]{2,1,0:T(8,128)} %bitcast.1, bf16[1,96,768]{2,1,0:T(8,128)(2,1)} %so_hbm.1, bf16[1,96,768]{2,1,0:T(8,128)(2,1)} %si_hbm.1, bf16[6,196,768]{2,1,0:T(8,128)(2,1)} %og_hbm.1, ...), custom_call_target="tpu_custom_call" | custom-call | tf_op jit(solution)/shard_map/moe_input_grad/pallas_call | solution.py:376
  21.8 1.3 %write_out.1 = (bf16[6,196,768]{2,1,0:T(8,128)(2,1)}, f32[1,768]{1,0:T(1,128)}) custom-call(bf16[6,196,768]{2,1,0:T(8,128)(2,1)S(1)} %get-tuple-element.4.ig_ref, f32[1,768]{1,0:T(1,128)S(1)} %get-tuple-element.5.rg_ref), custom_call_target="tpu_custom_call" | custom-call | tf_op jit(solution)/shard_map/write_out/pallas_call | solution.py:423
